TPU v7x, 32 devices: a whole 2x2x4 slice. The times are simulated.
32 devices in a mesh: tm: 8 (over y, x, core), chan: 4 (over z).
Axes of the slice: x: 2, y: 2, z: 4, core: 2. Of those that a mesh axis runs over, the one named last changes fastest.
Arguments:
- inputs: bfloat16 [4096, 8192], P('tm', 'chan'), may hold values from -52 to 52
- gate_logits: bfloat16 [4096, 8192], P(('tm', 'chan')), may hold values from -5 to 5
- step_sizes: bfloat16 [4096, 64], P('tm', 'chan'), may hold values from 0.3 to 28672, as said below
- decay_rates: float32 [8192], replicated, as said below
- skip_gain: float32 [8192], replicated, may hold values from 0.3 to 0.8
- norm_gain: float32 [8192], replicated, may hold values from 0.25 to 1.75
Outputs:
- outputs: bfloat16 [4096, 8192], P(('tm', 'chan'))
Inputs may be any that keep to these rules, and one draw needn't show every extreme that they name: `step_sizes`: every step size is positive. `decay_rates`: every rate is positive.
All inputs are finite; a program needn't handle non-finite values.
Results may differ from a plain program's by a relative error of at most 0.0049.
Values may be sent and summed in bfloat16 or wider, within the bound.
A program may use at most 64 MiB of HBM per device.

v0:
```python
import jax
import jax.numpy as jnp
from jax import lax
from jax.sharding import PartitionSpec as P

norm_epsilon = 1e-05


def entering(value, axis, combine, identity):
    count, mine = (lax.axis_size(axis), lax.axis_index(axis))
    everything = jax.tree.map(lambda part: lax.all_gather(part, axis), value)
    start = jax.tree.map(
        lambda part, zero: jnp.broadcast_to(jnp.asarray(zero, part.dtype), part.shape),
        value,
        identity,
    )

    def turn(k, before):
        reached = k < mine
        new = combine(before, jax.tree.map(lambda part: part[k], everything))
        return jax.tree.map(lambda a, b: jnp.where(reached, a, b), new, before)

    return lax.fori_loop(0, count, turn, start)


def combine_pairs(earlier, later):
    return (earlier[0] * later[0], later[0] * earlier[1] + later[1])


def widen(head_values, channels):
    head_count = head_values.shape[1]
    width_each = channels // head_count
    owner = lax.broadcasted_iota(jnp.int32, (head_count, channels), 1) // width_each
    column_head = lax.broadcasted_iota(jnp.int32, (head_count, channels), 0)
    spread_table = (owner == column_head).astype(jnp.float32)
    return jnp.dot(
        head_values,
        spread_table,
        precision=lax.Precision.HIGHEST,
        preferred_element_type=jnp.float32,
    )


def serial_rows(decays, drives, axis_pos):
    length = decays.shape[axis_pos]
    prod_list = []
    state_list = []
    prod_now = None
    state_now = None
    for index in range(length):
        decay_here = lax.index_in_dim(decays, index, axis_pos, keepdims=False)
        drive_here = lax.index_in_dim(drives, index, axis_pos, keepdims=False)
        if index == 0:
            prod_now = decay_here
            state_now = drive_here
        else:
            prod_now = prod_now * decay_here
            state_now = decay_here * state_now + drive_here
        prod_list.append(prod_now)
        state_list.append(state_now)
    return (jnp.stack(prod_list, axis=axis_pos), jnp.stack(state_list, axis=axis_pos))


def prefix_rows(decays, drives):
    length = decays.shape[0]
    channels = decays.shape[1]
    if length <= 8:
        return serial_rows(decays, drives, 0)
    group = 8
    groups = length // group
    grouped_decay = decays.reshape(groups, group, channels)
    grouped_drive = drives.reshape(groups, group, channels)
    inner_prod, inner_state = serial_rows(grouped_decay, grouped_drive, 1)
    outer_prod, outer_state = prefix_rows(inner_prod[:, -1, :], inner_state[:, -1, :])
    before_prod = jnp.concatenate([jnp.ones((1, channels), jnp.float32), outer_prod[:-1]], axis=0)
    before_state = jnp.concatenate(
        [jnp.zeros((1, channels), jnp.float32), outer_state[:-1]], axis=0
    )
    products = inner_prod * before_prod[:, None, :]
    states = inner_state + inner_prod * before_state[:, None, :]
    return (products.reshape(length, channels), states.reshape(length, channels))


def chain_time(end_decay, end_state):
    identity = (jnp.ones_like(end_decay), jnp.zeros_like(end_state))
    return entering((end_decay, end_state), "tm", combine_pairs, identity)[1]


def recurrence(block_inputs, block_steps, rates_here, skip_here, chain_fn):
    channels = block_inputs.shape[1]
    step_values = block_steps.astype(jnp.float32)
    widened = widen(step_values, channels) * rates_here[None, :]
    decays = jnp.exp(-widened)
    values = block_inputs.astype(jnp.float32)
    drives = jnp.sqrt(-jnp.expm1(-2.0 * widened)) * values
    products, local_states = prefix_rows(decays, drives)
    incoming = chain_fn(products[-1], local_states[-1])
    states = local_states + products * incoming[None, :]
    return (states + skip_here[None, :] * values).astype(jnp.bfloat16)


def normalize(mixed_rows, gate_logits, norm_gain):
    gated = mixed_rows.astype(jnp.float32) * jax.nn.silu(gate_logits.astype(jnp.float32))
    factor = lax.rsqrt(jnp.mean(gated * gated, axis=1, keepdims=True) + norm_epsilon)
    return (gated * factor * norm_gain[None, :]).astype(jnp.bfloat16)


def per_device(inputs, gate_logits, step_sizes, decay_rates, skip_gain, norm_gain):
    channels = inputs.shape[1]
    offset = lax.axis_index("chan") * channels
    rates_here = lax.dynamic_slice_in_dim(decay_rates, offset, channels, 0)
    skip_here = lax.dynamic_slice_in_dim(skip_gain, offset, channels, 0)
    mixed_rows = recurrence(inputs, step_sizes, rates_here, skip_here, chain_time)
    framed = lax.all_to_all(mixed_rows, "chan", split_axis=0, concat_axis=1, tiled=True)
    return normalize(framed, gate_logits, norm_gain)


def solution(mesh):
    in_specs = (P("tm", "chan"), P(("tm", "chan"), None), P("tm", "chan"), P(), P(), P())
    out_specs = P(("tm", "chan"), None)
    return jax.shard_map(
        per_device, mesh=mesh, in_specs=in_specs, out_specs=out_specs, check_vma=False
    )
```

profile of v0, /device:TPU:0, one launch (start us, length us, event | category | flops | bytes accessed | tf_op | source)
XLA Modules:
  0.0 148.7 jit_solution(7240075363780846964)
XLA Ops:
  0.0 0.0 copy-start
  0.0 0.7 dynamic_slice.20
  0.7 0.0 copy-done
  0.7 0.7 fusion.7
  1.5 0.0 copy-start.4
  1.5 0.9 exponential_bitcast_fusion
  2.4 0.6 copy-done.4
  3.1 2.7 %fusion = f32[64,8,2048]{2,1,0:T(8,128)S(1)} fusion(bf16[512,2048]{1,0:T(8,128)(2,1)S(1)} %copy-done.4, f32[2048,512]{0,1:T(8,128)S(1)} %fusion.7, f32[2048]{0:T(1024)S(1)} %dynamic_slice.20), kind=kLoop, calls=%fused_computation.7 | loop fusion | flops 5242880 | bytes 10493952 | tf_op jit(solution)/shard_map/reshape | solution.py:72
  5.8 6.3 %slice_multiply_fusion = (f32[64,1,2048]{2,1,0:T(1,128)S(1)}, f32[64,1,2048]{2,1,0:T(1,128)}, f32[64,1,2048]{2,1,0:T(1,128)}, f32[64,1,2048]{2,1,0:T(1,128)}, f3...) fusion(f32[64,8,2048]{2,1,0:T(8,128)S(1)} %exponential_bitcast_fusion), kind=kLoop, calls=%fused_computation.31 | loop fusion | flops 917504 | bytes 8388608 | tf_op jit(solution)/shard_map/mul | solution.py:57
  12.0 8.5 %slice_add_fusion = (f32[64,1,2048]{2,1,0:T(1,128)S(1)}, f32[64,1,2048]{2,1,0:T(1,128)}, f32[64,1,2048]{2,1,0:T(1,128)}, f32[64,1,2048]{2,1,0:T(1,128)}, f32[64,...) fusion(f32[64,8,2048]{2,1,0:T(8,128)S(1)} %fusion, ...), kind=kLoop, calls=%fused_computation.20 | loop fusion | flops 1835008 | bytes 12058624 | tf_op jit(solution)/shard_map/add | solution.py:58
  20.6 0.2 copy.19
  20.8 0.2 copy.18
  20.9 1.1 slice_multiply_fusion.7
  22.0 1.4 slice_add_fusion.7
  23.4 0.6 slice_bitcast_fusion.15
  24.0 0.1 fusion.13
  24.1 0.7 fusion.25
  24.8 2.3 %stack.10 = f32[8,8,2048]{2,1,0:T(8,128)} concatenate(f32[8,1,2048]{2,1,0:T(1,128)} %get-tuple-element.177, f32[8,1,2048]{2,1,0:T(1,128)} %get-tuple-element.153, f32[8,1,2048]{2,1,0:T(1,128)} %get-tuple-element.152, f32[8,1,2048]{2,1,0:T(1,128)} %get-tuple-element.151, f32[8,1,2048]{2,1,0:T(1,128)} %get-tuple-element.150, f32[8,1,2048]{2,1,0:T(1,128)} %get-tuple-element.149, ...), dimensions={1} | concatenate | bytes 1048576 | tf_op jit(solution)/shard_map/stack | solution.py:61
  27.1 2.2 %stack.11 = f32[8,8,2048]{2,1,0:T(8,128)} concatenate(f32[8,1,2048]{2,1,0:T(1,128)} %get-tuple-element.176, f32[8,1,2048]{2,1,0:T(1,128)} %get-tuple-element.146, f32[8,1,2048]{2,1,0:T(1,128)} %get-tuple-element.145, f32[8,1,2048]{2,1,0:T(1,128)} %get-tuple-element.144, f32[8,1,2048]{2,1,0:T(1,128)S(1)} %get-tuple-element.143, f32[8,1,2048]{2,1,0:T(1,128)S(1)} %get-tuple-element.142, ...), dimensions={1} | concatenate | bytes 1048576 | tf_op jit(solution)/shard_map/stack | solution.py:61
  29.3 0.8 concatenate.12
  30.1 0.9 concatenate.14
  31.0 1.3 multiply_bitcast_fusion.1
  32.3 0.8 concatenate.13
  33.1 0.8 concatenate.15
  34.0 11.9 %stack.8 = f32[64,8,2048]{2,1,0:T(8,128)} concatenate(f32[64,1,2048]{2,1,0:T(1,128)} %get-tuple-element.173, f32[64,1,2048]{2,1,0:T(1,128)} %get-tuple-element.167, f32[64,1,2048]{2,1,0:T(1,128)} %get-tuple-element.166, f32[64,1,2048]{2,1,0:T(1,128)} %get-tuple-element.165, f32[64,1,2048]{2,1,0:T(1,128)} %get-tuple-element.164, f32[64,1,2048]{2,1,0:T(1,128)} %get-tuple-element.163, ...), dimensions={1} | concatenate | bytes 8388608 | tf_op jit(solution)/shard_map/stack | solution.py:61
  45.9 0.0 copy-start.5
  45.9 12.0 %stack.9 = f32[64,8,2048]{2,1,0:T(8,128)} concatenate(f32[64,1,2048]{2,1,0:T(1,128)} %get-tuple-element.172, f32[64,1,2048]{2,1,0:T(1,128)} %get-tuple-element.160, f32[64,1,2048]{2,1,0:T(1,128)} %get-tuple-element.159, f32[64,1,2048]{2,1,0:T(1,128)} %get-tuple-element.158, f32[64,1,2048]{2,1,0:T(1,128)} %get-tuple-element.157, f32[64,1,2048]{2,1,0:T(1,128)} %get-tuple-element.156, ...), dimensions={1} | concatenate | bytes 8388608 | tf_op jit(solution)/shard_map/stack | solution.py:61
  57.8 0.0 copy-done.5
  57.8 0.0 dynamic-slice-start
  57.8 5.6 %multiply_bitcast_fusion = (f32[512,2048]{1,0:T(8,128)S(1)}, f32[512,2048]{1,0:T(8,128)S(1)}) fusion(f32[64,8,2048]{2,1,0:T(8,128)} %stack.9, f32[64,2048]{1,0:T(8,128)} %concatenate.15, f32[64,8,2048]{2,1,0:T(8,128)} %stack.8, f32[64,2048]{1,0:T(8,128)S(1)} %copy-done.5), kind=kLoop, calls=%fused_computation.17 | loop fusion | flops 3145728 | bytes 17825792 | tf_op jit(solution)/shard_map/mul | solution.py:79
  63.5 0.0 copy-start.1
  63.5 0.0 copy-start.2
  63.5 10.7 %all-gather.1 = f32[8,1,2048]{2,1,0:T(1,128)S(1)} all-gather(f32[1,1,2048]{2,1,0:T(1,128)S(1)} %slice_bitcast_fusion), channel_id=1, replica_groups=mesh['tm'=8,'chan'=4] {'tm'}, dimensions={0}, use_global_device_ids=true | all-gather | bytes 73728 | tf_op jit(solution)/shard_map/all_gather | solution.py:11
  74.3 0.0 copy-done.1
  74.3 0.0 copy-done.2
  74.3 9.2 %all-gather = f32[8,1,2048]{2,1,0:T(1,128)S(1)} all-gather(f32[1,1,2048]{2,1,0:T(1,128)S(1)} %slice_bitcast_fusion.1), channel_id=1, replica_groups=mesh['tm'=8,'chan'=4] {'tm'}, dimensions={0}, use_global_device_ids=true | all-gather | bytes 73728 | tf_op jit(solution)/shard_map/all_gather | solution.py:11
  83.6 0.7 while.14
  84.3 0.0 dynamic-slice-done
  84.3 4.7 %fusion.2 = bf16[512,2048]{1,0:T(8,128)(2,1)S(1)} fusion(bf16[512,2048]{1,0:T(8,128)(2,1)S(1)} %copy-done.4, f32[512,2048]{1,0:T(8,128)} %copy-done.2, f32[512,2048]{1,0:T(8,128)} %copy-done.1, f32[2048]{0:T(1024)S(1)} %dynamic-slice-done, f32[2048]{0:T(1024)S(1)} %get-tuple-element.99), kind=kLoop, calls=%fused_computation.9 | loop fusion | flops 6291456 | bytes 12599296 | tf_op jit(solution)/shard_map/convert_element_type | solution.py:99
  89.0 53.4 %all_to_all.13 = bf16[4,128,2048]{2,1,0:T(8,128)(2,1)S(1)} all-to-all(bf16[4,128,2048]{2,1,0:T(8,128)(2,1)S(1)} %bitcast.133), channel_id=1, replica_groups=mesh['tm'=8,'chan'=4] {'chan'}, dimensions={0} | all-to-all | bytes 4194304 | tf_op jit(solution)/shard_map/all_to_all | solution.py:114
  142.4 0.5 convert_bitcast_fusion
  142.9 0.0 copy-start.3
  142.9 0.3 copy.13
  143.2 0.0 copy-start.6
  143.2 1.3 copy-done.3
  144.5 1.5 multiply_reduce_fusion
  145.9 0.0 copy-done.6
  146.0 2.8 %multiply_convert_fusion = bf16[128,8192]{1,0:T(8,128)(2,1)} fusion(f32[8192]{0:T(1024)S(1)} %copy-done.6, f32[128]{0:T(128)S(1)} %add_rsqrt_fusion, f32[128,8192]{1,0:T(8,128)S(1)} %bitcast.132, bf16[128,8192]{1,0:T(8,128)(2,1)S(1)} %copy-done.3), kind=kLoop, calls=%fused_computation.15 | loop fusion | flops 9437184 | bytes 8421888 | tf_op jit(solution)/shard_map/convert_element_type | solution.py:105
  (27 shorter events, 0.3 us)
Async XLA Ops:
  0.0 0.7 copy-start
  1.5 1.6 %copy-start.4 = (bf16[512,2048]{1,0:T(8,128)(2,1)S(1)}, bf16[512,2048]{1,0:T(8,128)(2,1)}, u32[]{:S(2)}) copy-start(bf16[512,2048]{1,0:T(8,128)(2,1)} %param.8) | copy-start | bytes 6291460
  45.9 12.0 %copy-start.5 = (f32[64,2048]{1,0:T(8,128)S(1)}, f32[64,2048]{1,0:T(8,128)}, u32[]{:S(2)}) copy-start(f32[64,2048]{1,0:T(8,128)} %concatenate.13) | copy-start | bytes 1572868
  57.8 26.5 %dynamic-slice-start = ((f32[8192]{0:T(1024)}, s32[]{:T(128)}), f32[2048]{0:T(1024)S(1)}, s32[]{:S(2)}) async-start(f32[8192]{0:T(1024)} %param.12, s32[]{:T(128)} %select_n.32), calls=%async_computation.1 | async-start | bytes 16896 | tf_op jit(solution)/shard_map/dynamic_slice | solution.py:112
  63.5 10.8 %copy-start.1 = (f32[512,2048]{1,0:T(8,128)}, f32[512,2048]{1,0:T(8,128)S(1)}, u32[]{:S(2)}) copy-start(f32[512,2048]{1,0:T(8,128)S(1)} %get-tuple-element.170) | copy-start | bytes 12582916
  63.5 10.8 %copy-start.2 = (f32[512,2048]{1,0:T(8,128)}, f32[512,2048]{1,0:T(8,128)S(1)}, u32[]{:S(2)}) copy-start(f32[512,2048]{1,0:T(8,128)S(1)} %get-tuple-element.171) | copy-start | bytes 12582916
  142.9 1.6 %copy-start.3 = (bf16[128,8192]{1,0:T(8,128)(2,1)S(1)}, bf16[128,8192]{1,0:T(8,128)(2,1)}, u32[]{:S(2)}) copy-start(bf16[128,8192]{1,0:T(8,128)(2,1)} %param.9) | copy-start | bytes 6291460
  143.2 2.8 %copy-start.6 = (f32[8192]{0:T(1024)S(1)}, f32[8192]{0:T(1024)}, u32[]{:S(2)}) copy-start(f32[8192]{0:T(1024)} %param.13) | copy-start | bytes 98308
where the time goes:
time: 152 us; the launch traced here: 149 us
  blocking collectives  73.3 us (48%)
  other arithmetic  38.1 us (25%)
  local copies, waits for them, and re-layouts  35.8 us (24%)
    all_to_all x1, blocking collectives, per_device(): lax.all_to_all(mixed_rows, 'chan', split_axis=0, concat_axis=1, tiled=True)  53.4 us
    all_gather x2, blocking collectives, entering(): everything = jax.tree.map(lambda part: lax.all_gather(part, axis), value)  20 us
    another operation x2, local copies, waits for them, and re-layouts, serial_rows(): jnp.stack(prod_list, axis=axis_pos)  14.2 us
    another operation x2, local copies, waits for them, and re-layouts, serial_rows(): jnp.stack(state_list, axis=axis_pos)  14.2 us
    add x3, other arithmetic, serial_rows(): state_now = decay_here * state_now + drive_here  10 us
    mul x3, other arithmetic, serial_rows(): prod_now = prod_now * decay_here  8 us
    mul x2, other arithmetic, prefix_rows(): products = inner_prod * before_prod[:, None, :]  6.93 us
    convert_element_type x1, other arithmetic, recurrence(): return (states + skip_here[None, :] * values).astype(jnp.bfloat16)  4.67 us

commit v1 on v0

--- a/solution.py
+++ b/solution.py
@@ -111,7 +111,9 @@
     rates_here = lax.dynamic_slice_in_dim(decay_rates, offset, channels, 0)
     skip_here = lax.dynamic_slice_in_dim(skip_gain, offset, channels, 0)
     mixed_rows = recurrence(inputs, step_sizes, rates_here, skip_here, chain_time)
-    framed = lax.all_to_all(mixed_rows, "chan", split_axis=0, concat_axis=1, tiled=True)
+    shards = jnp.split(mixed_rows, lax.axis_size("chan"), axis=0)
+    received = lax.all_to_all(jnp.stack(shards), "chan", 0, 0)
+    framed = jnp.concatenate(received, axis=1)
     return normalize(framed, gate_logits, norm_gain)
 
 

time: 152 us -> 168 us (1.11)
  blocking collectives: 73.3 us -> 20 us
  waiting for transfers between devices: 0 us -> 45.6 us
  local copies, waits for them, and re-layouts: 35.8 us -> 45.8 us
  other arithmetic: 38.1 us -> 47.3 us
  starting transfers between devices: 0 us -> 4.87 us
    all_to_all x1 -> x0, blocking collectives: 53.4 us -> none  [per_device(): lax.all_to_all(mixed_rows, 'chan', split_axis=0, concat_axis=1, tiled=True)]
    all_to_all x0 -> x1, waiting for transfers between devices: none -> 45.6 us  [per_device(): received = lax.all_to_all(jnp.stack(shards), 'chan', 0, 0)]
    convert_element_type x1, local copies, waits for them, and re-layouts: 0.27 us -> 5.37 us  [normalize(): mixed_rows.astype(jnp.float32)]
    all_to_all x0 -> x1, starting transfers between devices: none -> 4.87 us  [per_device(): received = lax.all_to_all(jnp.stack(shards), 'chan', 0, 0)]
    convert_element_type x0 -> x1, local copies, waits for them, and re-layouts: none -> 4.06 us  [normalize(): return (gated * factor * norm_gain[None, :]).astype(jnp.bfloat16)]
    convert_element_type x0 -> x1, other arithmetic: none -> 4.06 us  [normalize(): mixed_rows.astype(jnp.float32)]
    reduce_sum x1, other arithmetic: 1.45 us -> 3.78 us  [normalize(): jnp.mean(gated * gated, axis=1, keepdims=True) + norm_epsilon]
    unnamed x20 -> x23, local copies, waits for them, and re-layouts: 2.35 us -> 4.28 us
  transfers between devices with their start and end apart: 0 -> 1, of which waited for: 0 -> 1; matrix products, arithmetic and copies ran while one was open for 0% -> 2% of each run, Pallas kernels for 0% -> 0%
where the time goes in v1:
time: 168 us; the launch traced here: 165 us
  other arithmetic  47.3 us (28%)
  local copies, waits for them, and re-layouts  45.8 us (27%)
  waiting for transfers between devices  45.6 us (27%)
  blocking collectives  20 us (12%)
  starting transfers between devices  4.87 us (3%)
    all_to_all x1, waiting for transfers between devices, per_device(): received = lax.all_to_all(jnp.stack(shards), 'chan', 0, 0)  45.6 us
    all_gather x2, blocking collectives, entering(): everything = jax.tree.map(lambda part: lax.all_gather(part, axis), value)  20 us
    another operation x2, local copies, waits for them, and re-layouts, serial_rows(): jnp.stack(prod_list, axis=axis_pos)  14.2 us
    another operation x2, local copies, waits for them, and re-layouts, serial_rows(): jnp.stack(state_list, axis=axis_pos)  14.2 us
    add x3, other arithmetic, serial_rows(): state_now = decay_here * state_now + drive_here  10 us
    mul x3, other arithmetic, serial_rows(): prod_now = prod_now * decay_here  7.97 us
    mul x2, other arithmetic, prefix_rows(): products = inner_prod * before_prod[:, None, :]  6.93 us
    convert_element_type x1, local copies, waits for them, and re-layouts, normalize(): mixed_rows.astype(jnp.float32)  5.37 us
  transfers between devices with their start and end apart: 1, of which 1 were waited for; matrix products, arithmetic and copies ran while one was open for 2% of the time, Pallas kernels for 0%

profile of v1, /device:TPU:0, one launch (start us, length us, event | category | flops | bytes accessed | tf_op | source)
XLA Modules:
  0.0 164.9 jit_solution(15479669842930217423)
XLA Ops:
  0.0 0.0 copy-start
  0.0 0.7 dynamic_slice.20
  0.7 0.0 copy-done
  0.7 0.7 fusion.7
  1.5 0.0 copy-start.5
  1.5 0.9 exponential_bitcast_fusion
  2.4 0.6 copy-done.5
  3.1 2.7 %fusion = f32[64,8,2048]{2,1,0:T(8,128)S(1)} fusion(bf16[512,2048]{1,0:T(8,128)(2,1)S(1)} %copy-done.5, f32[2048,512]{0,1:T(8,128)S(1)} %fusion.7, f32[2048]{0:T(1024)S(1)} %dynamic_slice.20), kind=kLoop, calls=%fused_computation.7 | loop fusion | flops 5242880 | bytes 10493952 | tf_op jit(solution)/shard_map/reshape | solution.py:72
  5.8 6.3 %slice_multiply_fusion = (f32[64,1,2048]{2,1,0:T(1,128)S(1)}, f32[64,1,2048]{2,1,0:T(1,128)}, f32[64,1,2048]{2,1,0:T(1,128)}, f32[64,1,2048]{2,1,0:T(1,128)}, f3...) fusion(f32[64,8,2048]{2,1,0:T(8,128)S(1)} %exponential_bitcast_fusion), kind=kLoop, calls=%fused_computation.36 | loop fusion | flops 917504 | bytes 8388608 | tf_op jit(solution)/shard_map/mul | solution.py:57
  12.0 8.5 %slice_add_fusion = (f32[64,1,2048]{2,1,0:T(1,128)S(1)}, f32[64,1,2048]{2,1,0:T(1,128)}, f32[64,1,2048]{2,1,0:T(1,128)}, f32[64,1,2048]{2,1,0:T(1,128)}, f32[64,...) fusion(f32[64,8,2048]{2,1,0:T(8,128)S(1)} %fusion, ...), kind=kLoop, calls=%fused_computation.25 | loop fusion | flops 1835008 | bytes 12058624 | tf_op jit(solution)/shard_map/add | solution.py:58
  20.6 0.2 copy.22
  20.8 0.2 copy.21
  20.9 1.1 slice_multiply_fusion.7
  22.0 1.4 slice_add_fusion.7
  23.4 0.1 fusion.13
  23.5 0.6 fusion.25
  24.1 2.3 %stack.20 = f32[8,8,2048]{2,1,0:T(8,128)} concatenate(f32[8,1,2048]{2,1,0:T(1,128)} %get-tuple-element.181, f32[8,1,2048]{2,1,0:T(1,128)} %get-tuple-element.153, f32[8,1,2048]{2,1,0:T(1,128)} %get-tuple-element.152, f32[8,1,2048]{2,1,0:T(1,128)} %get-tuple-element.151, f32[8,1,2048]{2,1,0:T(1,128)} %get-tuple-element.150, f32[8,1,2048]{2,1,0:T(1,128)} %get-tuple-element.149, ...), dimensions={1} | concatenate | bytes 1048576 | tf_op jit(solution)/shard_map/stack | solution.py:61
  26.4 2.2 %stack.21 = f32[8,8,2048]{2,1,0:T(8,128)} concatenate(f32[8,1,2048]{2,1,0:T(1,128)} %get-tuple-element.180, f32[8,1,2048]{2,1,0:T(1,128)} %get-tuple-element.146, f32[8,1,2048]{2,1,0:T(1,128)} %get-tuple-element.145, f32[8,1,2048]{2,1,0:T(1,128)} %get-tuple-element.144, f32[8,1,2048]{2,1,0:T(1,128)S(1)} %get-tuple-element.143, f32[8,1,2048]{2,1,0:T(1,128)S(1)} %get-tuple-element.142, ...), dimensions={1} | concatenate | bytes 1048576 | tf_op jit(solution)/shard_map/stack | solution.py:61
  28.7 0.1 concatenate.12
  28.8 0.9 concatenate.14
  29.7 1.3 multiply_bitcast_fusion.1
  31.0 0.9 concatenate.13
  31.8 0.8 concatenate.15
  32.7 11.9 %stack.18 = f32[64,8,2048]{2,1,0:T(8,128)} concatenate(f32[64,1,2048]{2,1,0:T(1,128)} %get-tuple-element.173, f32[64,1,2048]{2,1,0:T(1,128)} %get-tuple-element.167, f32[64,1,2048]{2,1,0:T(1,128)} %get-tuple-element.166, f32[64,1,2048]{2,1,0:T(1,128)} %get-tuple-element.165, f32[64,1,2048]{2,1,0:T(1,128)} %get-tuple-element.164, f32[64,1,2048]{2,1,0:T(1,128)} %get-tuple-element.163, ...), dimensions={1} | concatenate | bytes 8388608 | tf_op jit(solution)/shard_map/stack | solution.py:61
  44.5 0.0 copy-start.6
  44.5 12.0 %stack.19 = f32[64,8,2048]{2,1,0:T(8,128)} concatenate(f32[64,1,2048]{2,1,0:T(1,128)} %get-tuple-element.172, f32[64,1,2048]{2,1,0:T(1,128)} %get-tuple-element.160, f32[64,1,2048]{2,1,0:T(1,128)} %get-tuple-element.159, f32[64,1,2048]{2,1,0:T(1,128)} %get-tuple-element.158, f32[64,1,2048]{2,1,0:T(1,128)} %get-tuple-element.157, f32[64,1,2048]{2,1,0:T(1,128)} %get-tuple-element.156, ...), dimensions={1} | concatenate | bytes 8388608 | tf_op jit(solution)/shard_map/stack | solution.py:61
  56.5 0.0 copy-done.6
  56.5 0.0 dynamic-slice-start
  56.6 5.6 %multiply_bitcast_fusion = (f32[512,2048]{1,0:T(8,128)S(1)}, f32[512,2048]{1,0:T(8,128)S(1)}) fusion(f32[64,8,2048]{2,1,0:T(8,128)} %stack.19, f32[64,2048]{1,0:T(8,128)} %concatenate.15, f32[64,8,2048]{2,1,0:T(8,128)} %stack.18, f32[64,2048]{1,0:T(8,128)S(1)} %copy-done.6), kind=kLoop, calls=%fused_computation.17 | loop fusion | flops 3145728 | bytes 17825792 | tf_op jit(solution)/shard_map/mul | solution.py:79
  62.2 0.0 copy-start.3
  62.2 0.0 copy-start.4
  62.2 10.7 %all-gather.1 = f32[8,1,2048]{2,1,0:T(1,128)S(1)} all-gather(f32[1,1,2048]{2,1,0:T(1,128)S(1)} %slice_bitcast_fusion.4), channel_id=1, replica_groups=mesh['tm'=8,'chan'=4] {'tm'}, dimensions={0}, use_global_device_ids=true | all-gather | bytes 73728 | tf_op jit(solution)/shard_map/all_gather | solution.py:11
  73.0 0.0 copy-done.3
  73.0 0.0 copy-done.4
  73.0 9.2 %all-gather = f32[8,1,2048]{2,1,0:T(1,128)S(1)} all-gather(f32[1,1,2048]{2,1,0:T(1,128)S(1)} %slice_bitcast_fusion.5), channel_id=1, replica_groups=mesh['tm'=8,'chan'=4] {'tm'}, dimensions={0}, use_global_device_ids=true | all-gather | bytes 73728 | tf_op jit(solution)/shard_map/all_gather | solution.py:11
  82.3 0.7 while.14
  83.0 0.0 dynamic-slice-done
  83.0 4.7 %fusion.2 = bf16[512,2048]{1,0:T(8,128)(2,1)S(1)} fusion(bf16[512,2048]{1,0:T(8,128)(2,1)S(1)} %copy-done.5, f32[512,2048]{1,0:T(8,128)} %copy-done.4, f32[512,2048]{1,0:T(8,128)} %copy-done.3, f32[2048]{0:T(1024)S(1)} %dynamic-slice-done, f32[2048]{0:T(1024)S(1)} %get-tuple-element.99), kind=kLoop, calls=%fused_computation.9 | loop fusion | flops 6291456 | bytes 12599296 | tf_op jit(solution)/shard_map/convert_element_type | solution.py:99
  87.7 0.1 slice_bitcast_fusion.3
  87.8 1.6 pad_maximum_fusion
  89.4 4.9 %all-to-all-start = ((bf16[4,128,2048]{2,1,0:T(8,128)(2,1)}), bf16[4,128,2048]{2,1,0:T(8,128)(2,1)}, u32[]{:S(2)}, u32[]{:S(2)}) async-start(bf16[4,128,2048]{2,1,0:T(8,128)(2,1)} %pad_maximum_fusion), calls=%async_computation | async-start | bytes 4194304 | tf_op jit(solution)/shard_map/all_to_all | solution.py:115
  94.3 3.2 %copy.11 = bf16[128,8192]{0,1:T(8,128)(2,1)S(1)} copy(bf16[128,8192]{1,0:T(8,128)(2,1)} %param.9) | data formatting | bytes 4194304 | tf_op args[1]
  97.5 45.6 %all-to-all-done = bf16[4,128,2048]{2,1,0:T(8,128)(2,1)} async-done(((bf16[4,128,2048]{2,1,0:T(8,128)(2,1)}), bf16[4,128,2048]{2,1,0:T(8,128)(2,1)}, u32[]{:S(2)}, u32[]{:S(2)}) %all-to-all-start) | async-done | bytes 2097184 | tf_op jit(solution)/shard_map/all_to_all | solution.py:115
  143.1 4.1 %convert_bitcast_fusion = f32[128,4,2048]{2,0,1:T(8,128)} fusion(bf16[4,128,2048]{2,1,0:T(8,128)(2,1)} %all-to-all-done), kind=kLoop, calls=%fused_computation.14 | loop fusion | flops 1048576 | bytes 6291456 | tf_op jit(solution)/shard_map/convert_element_type | solution.py:103
  147.2 5.4 %copy.10 = f32[128,4,2048]{0,2,1:T(8,128)} copy(f32[128,4,2048]{2,0,1:T(8,128)} %convert_bitcast_fusion) | data formatting | bytes 8388608 | tf_op jit(solution)/shard_map/convert_element_type | solution.py:103
  152.5 0.0 copy-start.2
  152.5 0.0 copy-start.7
  152.5 3.8 %multiply_reduce_fusion = f32[128]{0:T(128)S(1)} fusion(bf16[128,8192]{0,1:T(8,128)(2,1)S(1)} %copy.11, f32[128,4,2048]{0,2,1:T(8,128)} %copy.10), kind=kLoop, calls=%fused_computation.16 | loop fusion | flops 8388480 | bytes 6291968 | tf_op jit(solution)/shard_map/reduce_sum | solution.py:104
  156.3 0.0 copy-done.2
  156.3 0.0 copy-done.7
  156.3 0.0 copy-start.1
  156.4 4.5 %multiply_convert_fusion = bf16[128,8192]{0,1:T(8,128)(2,1)} fusion(f32[8192]{0:T(1024)S(1)} %copy-done.7, f32[128]{0:T(128)S(1)} %add_rsqrt_fusion, bf16[128,8192]{0,1:T(8,128)(2,1)S(1)} %copy.11, f32[128,4,2048]{0,2,1:T(8,128)S(1)} %copy-done.2), kind=kLoop, calls=%fused_computation.15 | loop fusion | flops 9437184 | bytes 8421888 | tf_op jit(solution)/shard_map/convert_element_type | solution.py:105
  160.9 4.1 %copy.12 = bf16[128,8192]{1,0:T(8,128)(2,1)} copy(bf16[128,8192]{0,1:T(8,128)(2,1)} %multiply_convert_fusion) | data formatting | bytes 4194304 | tf_op jit(solution)/shard_map/convert_element_type | solution.py:105
  164.9 0.0 copy-done.1
  (28 shorter events, 0.3 us)
Async XLA Ops:
  0.0 0.7 copy-start
  1.5 1.6 copy-start.5
  44.5 12.0 %copy-start.6 = (f32[64,2048]{1,0:T(8,128)S(1)}, f32[64,2048]{1,0:T(8,128)}, u32[]{:S(2)}) copy-start(f32[64,2048]{1,0:T(8,128)} %concatenate.13) | copy-start | bytes 1572868
  56.5 26.5 %dynamic-slice-start = ((f32[8192]{0:T(1024)}, s32[]{:T(128)}), f32[2048]{0:T(1024)S(1)}, s32[]{:S(2)}) async-start(f32[8192]{0:T(1024)} %param.12, s32[]{:T(128)} %select_n.32), calls=%async_computation.1 | async-start | bytes 16896 | tf_op jit(solution)/shard_map/dynamic_slice | solution.py:112
  62.2 10.8 %copy-start.3 = (f32[512,2048]{1,0:T(8,128)}, f32[512,2048]{1,0:T(8,128)S(1)}, u32[]{:S(2)}) copy-start(f32[512,2048]{1,0:T(8,128)S(1)} %get-tuple-element.170) | copy-start | bytes 12582916
  62.2 10.8 %copy-start.4 = (f32[512,2048]{1,0:T(8,128)}, f32[512,2048]{1,0:T(8,128)S(1)}, u32[]{:S(2)}) copy-start(f32[512,2048]{1,0:T(8,128)S(1)} %get-tuple-element.171) | copy-start | bytes 12582916
  89.4 53.7 %all-to-all-start = ((bf16[4,128,2048]{2,1,0:T(8,128)(2,1)}), bf16[4,128,2048]{2,1,0:T(8,128)(2,1)}, u32[]{:S(2)}, u32[]{:S(2)}) async-start(bf16[4,128,2048]{2,1,0:T(8,128)(2,1)} %pad_maximum_fusion), calls=%async_computation | async-start | bytes 4194304 | tf_op jit(solution)/shard_map/all_to_all | solution.py:115
  152.5 3.8 %copy-start.2 = (f32[128,4,2048]{0,2,1:T(8,128)S(1)}, f32[128,4,2048]{0,2,1:T(8,128)}, u32[]{:S(2)}) copy-start(f32[128,4,2048]{0,2,1:T(8,128)} %copy.10) | copy-start | bytes 12582916
  152.5 3.8 %copy-start.7 = (f32[8192]{0:T(1024)S(1)}, f32[8192]{0:T(1024)}, u32[]{:S(2)}) copy-start(f32[8192]{0:T(1024)} %param.13) | copy-start | bytes 98308
  156.3 8.6 %copy-start.1 = (bf16[512,16]{0,1:T(8,128)(2,1)S(1)}, bf16[512,16]{0,1:T(8,128)(2,1)}, u32[]{:S(2)}) copy-start(bf16[512,16]{0,1:T(8,128)(2,1)} %param.10) | copy-start | bytes 49156
